TPU v7x, 32 devices: a whole 2x2x4 slice. The times are simulated.
32 devices in a mesh: bank: 4 (over y, core), zero: 8 (over z, x).
Axes of the slice: x: 2, y: 2, z: 4, core: 2. Of those that a mesh axis runs over, the one named last changes fastest.
Arguments:
- train_gate: float32 [128, 2048, 768], P('bank', 'zero'), may hold values from -0.1875 to 0.1875
- other_gate: bfloat16 [128, 2048, 768], P('bank', 'zero'), may hold values from -0.0625 to 0.0625
- train_up: float32 [128, 2048, 768], P('bank', 'zero'), may hold values from -0.1875 to 0.1875
- other_up: bfloat16 [128, 2048, 768], P('bank', 'zero'), may hold values from -0.0625 to 0.0625
- router_weight: float32 [2048, 128], P('zero', 'bank'), may hold values from -0.125 to 0.125
- router_gain: float32 [2048], P('zero'), may hold values from 0.25 to 1.75
Outputs:
- ready_gate: bfloat16 [128, 2048, 768], P(('bank', 'zero'))
- ready_up: bfloat16 [128, 2048, 768], P(('bank', 'zero'))
- scale_gate: float32 [128, 768], P(('bank', 'zero'))
- scale_up: float32 [128, 768], P(('bank', 'zero'))
- serve_router: bfloat16 [2048, 128], replicated
All inputs are finite; a program needn't handle non-finite values.
Results may differ from a plain program's by a relative error of at most 0.0075.
Values may be sent and summed in bfloat16 or wider, within the bound.
A program may use at most 192 MiB of HBM per device.

v0:
```python
import jax
import jax.numpy as jnp
from jax import lax
from jax.sharding import PartitionSpec as P


def body(train_gate, other_gate, train_up, other_up, router_weight, router_gain):
    latest_gate = train_gate + other_gate.astype(jnp.float32)
    latest_up = train_up + other_up.astype(jnp.float32)
    total_gate, total_up = (
        lax.psum(jnp.sum(latest_gate * latest_gate, axis=1).astype(jnp.bfloat16), "zero").astype(
            jnp.float32
        ),
        lax.psum(jnp.sum(latest_up * latest_up, axis=1).astype(jnp.bfloat16), "zero").astype(
            jnp.float32
        ),
    )
    scale_gate = jnp.sqrt(total_gate)
    scale_up = jnp.sqrt(total_up)
    narrow_gate, narrow_up = (
        (latest_gate / jnp.expand_dims(scale_gate, 1)).astype(jnp.bfloat16),
        (latest_up / jnp.expand_dims(scale_up, 1)).astype(jnp.bfloat16),
    )
    ready_gate, ready_up = (
        lax.all_to_all(narrow_gate, "zero", split_axis=0, concat_axis=1, tiled=True),
        lax.all_to_all(narrow_up, "zero", split_axis=0, concat_axis=1, tiled=True),
    )
    scale_gate = lax.dynamic_slice_in_dim(
        scale_gate, lax.axis_index("zero") * ready_gate.shape[0], ready_gate.shape[0], axis=0
    )
    scale_up = lax.dynamic_slice_in_dim(
        scale_up, lax.axis_index("zero") * ready_up.shape[0], ready_up.shape[0], axis=0
    )
    part_router = (router_weight * router_gain[:, None]).astype(jnp.bfloat16)
    row_router = lax.all_gather(part_router, "zero", axis=0, tiled=True)
    serve_router = lax.all_gather(row_router, "bank", axis=1, tiled=True)
    return (ready_gate, ready_up, scale_gate, scale_up, serve_router)


def solution(mesh):
    placed = (
        P("bank", "zero", None),
        P("bank", "zero", None),
        P("bank", "zero", None),
        P("bank", "zero", None),
        P("zero", "bank"),
        P("zero"),
    )
    return jax.shard_map(
        body,
        mesh=mesh,
        in_specs=placed,
        out_specs=(
            P(("bank", "zero"), None, None),
            P(("bank", "zero"), None, None),
            P(("bank", "zero"), None),
            P(("bank", "zero"), None),
            P(),
        ),
        check_vma=False,
    )
```

profile of v0, /device:TPU:0, one launch (start us, length us, event | category | flops | bytes accessed | tf_op | source)
XLA Modules:
  0.0 735.0 jit_solution(10002931296781212974)
XLA Ops:
  7.2 0.0 all-reduce.3.cloned.1.call-start
  7.2 25.1 %multiply_reduce_fusion = (bf16[32,768]{1,0:T(8,128)(2,1)}, bf16[32,768]{1,0:T(8,128)(2,1)}) fusion(f32[32,256,768]{2,1,0:T(8,128)} %param.8, bf16[32,256,768]{2,1,0:T(8,128)(2,1)} %param.9, f32[32,256,768]{2,1,0:T(8,128)} %param.6, bf16[32,256,768]{2,1,0:T(8,128)(2,1)} %param.7), kind=kLoop, calls=%fused_computation.1 | loop fusion | flops 50282496 | bytes 75595776 | tf_op jit(solution)/shard_map/reduce_sum | solution.py:14
  32.4 0.0 all-reduce.3.cloned.1.call-update
  32.4 73.3 %all-reduce.3.cloned.1.call-done = (bf16[32,768]{1,0:T(8,128)(2,1)}, bf16[32,768]{1,0:T(8,128)(2,1)}) async-done(((bf16[32,768]{1,0:T(8,128)(2,1)}, bf16[32,768]{1,0:T(8,128)(2,1)}), (bf16[32,768]{1,0:T(8,128)(2,1)}, bf16[32,768]{1,0:T(8,128)(2,1)})) %all-reduce.3.cloned.1.call-update) | async-done | bytes 98320 | tf_op jit(solution)/shard_map/psum | solution.py:11
  105.7 0.8 convert_sqrt_fusion.1
  106.6 17.2 %divide_convert_fusion.1 = bf16[32,256,768]{2,1,0:T(8,128)(2,1)} fusion(f32[32,256,768]{2,1,0:T(8,128)} %param.6, bf16[32,256,768]{2,1,0:T(8,128)(2,1)} %param.7, f32[32,768]{1,0:T(8,128)S(1)} %convert_sqrt_fusion.1), kind=kLoop, calls=%fused_computation.3 | loop fusion | flops 25165824 | bytes 50429952 | tf_op jit(solution)/shard_map/convert_element_type | solution.py:21
  123.8 0.0 copy-start
  123.8 5.5 all-to-all-start
  129.3 0.0 copy-done
  129.3 17.4 %divide_convert_fusion = bf16[32,256,768]{2,1,0:T(8,128)(2,1)} fusion(f32[32,256,768]{2,1,0:T(8,128)} %param.8, bf16[32,256,768]{2,1,0:T(8,128)(2,1)} %param.9, f32[32,768]{1,0:T(8,128)S(1)} %convert_sqrt_fusion), kind=kLoop, calls=%fused_computation | loop fusion | flops 25165824 | bytes 50429952 | tf_op jit(solution)/shard_map/convert_element_type | solution.py:22
  146.7 0.0 copy-start.1
  146.7 0.0 copy-start.2
  146.7 253.8 %all-to-all-done = bf16[32,256,768]{2,1,0:T(8,128)(2,1)} async-done(((bf16[32,256,768]{2,1,0:T(8,128)(2,1)}), bf16[32,256,768]{2,1,0:T(8,128)(2,1)}, u32[]{:S(2)}, u32[]{:S(2)}) %all-to-all-start) | async-done | bytes 12582944 | tf_op jit(solution)/shard_map/all_to_all | solution.py:25
  400.5 5.4 all-to-all-start.1
  405.9 0.0 copy-done.1
  405.9 0.0 copy-done.2
  405.9 291.6 %all_gather.6 = bf16[2048,32]{0,1:T(8,128)(2,1)S(1)} all-gather(bf16[256,32]{0,1:T(8,128)(2,1)S(1)} %multiply_convert_fusion), channel_id=1, replica_groups=mesh['bank'=4,'zero'=8] {'zero'}, dimensions={0}, use_global_device_ids=true | all-gather | bytes 147456 | tf_op jit(solution)/shard_map/all_gather | solution.py:35
  697.5 7.1 all_gather.7
  704.6 1.0 copy.16
  705.6 0.6 constant_dynamic-slice_fusion
  706.2 0.6 constant_dynamic-slice_fusion.1
  706.8 10.7 %copy.14 = bf16[8,4,256,768]{3,2,0,1:T(8,128)(2,1)} copy(bf16[8,4,256,768]{3,2,1,0:T(8,128)(2,1)} %bitcast) | data formatting | bytes 25165824 | tf_op jit(solution)/shard_map/all_to_all | solution.py:25
  717.5 0.0 all-to-all-done.1
  717.5 10.7 %copy.15 = bf16[8,4,256,768]{3,2,0,1:T(8,128)(2,1)} copy(bf16[8,4,256,768]{3,2,1,0:T(8,128)(2,1)} %bitcast.3) | data formatting | bytes 25165824 | tf_op jit(solution)/shard_map/all_to_all | solution.py:26
  (2 shorter events, 0.0 us)
Async XLA Ops:
  7.2 98.6 %all-reduce.3.cloned.1.call-start = ((), (), s32[]{:S(2)}) async-start(), calls=%async_computation.2 | async-start | bytes 196608 | tf_op jit(solution)/shard_map/psum | solution.py:11
  123.8 5.5 copy-start
  123.8 276.7 %all-to-all-start = ((bf16[32,256,768]{2,1,0:T(8,128)(2,1)}), bf16[32,256,768]{2,1,0:T(8,128)(2,1)}, u32[]{:S(2)}, u32[]{:S(2)}) async-start(bf16[32,256,768]{2,1,0:T(8,128)(2,1)} %divide_convert_fusion.1), calls=%async_computation | async-start | bytes 25165824 | tf_op jit(solution)/shard_map/all_to_all | solution.py:25
  146.7 259.2 %copy-start.1 = (f32[256,32]{0,1:T(8,128)S(1)}, f32[256,32]{0,1:T(8,128)}, u32[]{:S(2)}) copy-start(f32[256,32]{0,1:T(8,128)} %param.10) | copy-start | bytes 98308
  146.7 259.2 %copy-start.2 = (f32[256]{0:T(256)S(1)}, f32[256]{0:T(256)}, u32[]{:S(2)}) copy-start(f32[256]{0:T(256)} %param.11) | copy-start | bytes 3076
  400.5 317.0 %all-to-all-start.1 = ((bf16[32,256,768]{2,1,0:T(8,128)(2,1)}), bf16[32,256,768]{2,1,0:T(8,128)(2,1)}, u32[]{:S(2)}, u32[]{:S(2)}) async-start(bf16[32,256,768]{2,1,0:T(8,128)(2,1)} %divide_convert_fusion), calls=%async_computation.1 | async-start | bytes 25165824 | tf_op jit(solution)/shard_map/all_to_all | solution.py:26
Sparse Core Ops, SparseCore 0:
  32.5 73.1 all-reduce.2
where the time goes:
time: 735 us
  waiting for transfers between devices  327 us (44%)
  blocking collectives  299 us (41%)
  other arithmetic  60.6 us (8%)
  local copies, waits for them, and re-layouts  23.6 us (3%)
  between operations  14.1 us (2%)
  starting transfers between devices  10.9 us (1%)
    all_gather x1, blocking collectives, body(): row_router = lax.all_gather(part_router, 'zero', axis=0, tiled=True)  292 us
    all_to_all x1, waiting for transfers between devices, body(): lax.all_to_all(narrow_gate, 'zero', split_axis=0, concat_axis=1, tiled=True)  254 us
    psum x1, waiting for transfers between devices, body(): lax.psum(jnp.sum(latest_gate * latest_gate, axis=1).astype(jnp.bfloat16),...  73.3 us
    reduce_sum x1, other arithmetic, body(): jnp.sum(latest_up * latest_up, axis=1).astype(jnp.bfloat16)  25.1 us
    convert_element_type x1, other arithmetic, body(): (latest_up / jnp.expand_dims(scale_up, 1)).astype(jnp.bfloat16)  17.4 us
    convert_element_type x1, other arithmetic, body(): (latest_gate / jnp.expand_dims(scale_gate, 1)).astype(jnp.bfloat16)  17.2 us
  transfers between devices with their start and end apart: 3, of which 2 were waited for; matrix products, arithmetic and copies ran while one was open for 4% of the time, Pallas kernels for 0%

commit v1 on v0

--- a/solution.py
+++ b/solution.py
@@ -8,9 +8,10 @@
     latest_gate = train_gate + other_gate.astype(jnp.float32)
     latest_up = train_up + other_up.astype(jnp.float32)
     total_gate, total_up = (
-        lax.psum(jnp.sum(latest_gate * latest_gate, axis=1).astype(jnp.bfloat16), "zero").astype(
-            jnp.float32
-        ),
+        jnp.sum(
+            lax.all_gather(jnp.sum(latest_gate * latest_gate, axis=1).astype(jnp.bfloat16), "zero"),
+            axis=0,
+        ).astype(jnp.float32),
         lax.psum(jnp.sum(latest_up * latest_up, axis=1).astype(jnp.bfloat16), "zero").astype(
             jnp.float32
         ),

time: 735 us -> 700 us (0.952)
  waiting for transfers between devices: 327 us -> 0.01 us
  blocking collectives: 299 us -> 604 us
  between operations: 14.1 us -> 0.71 us
    psum x0 -> x1, blocking collectives: none -> 278 us  [body(): lax.psum(jnp.sum(latest_up * latest_up, axis=1).astype(jnp.bfloat16), 'ze...]
    all_to_all x1, waiting for transfers between devices: 254 us -> 0.01 us  [body(): lax.all_to_all(narrow_gate, 'zero', split_axis=0, concat_axis=1, tiled=True)]
    psum x1 -> x0, waiting for transfers between devices: 73.3 us -> none  [body(): lax.psum(jnp.sum(latest_gate * latest_gate, axis=1).astype(jnp.bfloat16),...]
    all_gather x0 -> x1, blocking collectives: none -> 32.8 us  [body(): lax.all_gather(jnp.sum(latest_gate * latest_gate, axis=1).astype(jnp.bflo...]
    reduce_sum x0 -> x2, other arithmetic: none -> 12.9 us  [the longest x1 12.8 us: body(): jnp.sum(latest_gate * latest_gate, axis=1).astype(jnp.bfloat16)]
    reduce_sum x1, other arithmetic: 25.1 us -> 12.8 us  [body(): jnp.sum(latest_up * latest_up, axis=1).astype(jnp.bfloat16)]
  transfers between devices with their start and end apart: 3 -> 2, of which waited for: 2 -> 0; matrix products, arithmetic and copies ran while one was open for 4% -> 6% of each run, Pallas kernels for 0% -> 0%
where the time goes in v1:
time: 700 us
  blocking collectives  604 us (86%)
  other arithmetic  60.5 us (9%)
  local copies, waits for them, and re-layouts  23.6 us (3%)
  starting transfers between devices  11.1 us (2%)
    all_gather x1, blocking collectives, body(): row_router = lax.all_gather(part_router, 'zero', axis=0, tiled=True)  286 us
    psum x1, blocking collectives, body(): lax.psum(jnp.sum(latest_up * latest_up, axis=1).astype(jnp.bfloat16), 'ze...  278 us
    all_gather x1, blocking collectives, body(): lax.all_gather(jnp.sum(latest_gate * latest_gate, axis=1).astype(jnp.bflo...  32.8 us
    convert_element_type x1, other arithmetic, body(): (latest_up / jnp.expand_dims(scale_up, 1)).astype(jnp.bfloat16)  17.4 us
    convert_element_type x1, other arithmetic, body(): (latest_gate / jnp.expand_dims(scale_gate, 1)).astype(jnp.bfloat16)  17.2 us
  transfers between devices with their start and end apart: 2, of which 0 were waited for; matrix products, arithmetic and copies ran while one was open for 6% of the time, Pallas kernels for 0%

profile of v1, /device:TPU:0, one launch (start us, length us, event | category | flops | bytes accessed | tf_op | source)
XLA Modules:
  0.0 699.6 jit_solution(13801321754549594710)
XLA Ops:
  0.6 12.8 %multiply_reduce_fusion.1 = bf16[32,768]{1,0:T(8,128)(2,1)S(1)} fusion(f32[32,256,768]{2,1,0:T(8,128)} %param.6, bf16[32,256,768]{2,1,0:T(8,128)(2,1)} %param.7), kind=kLoop, calls=%fused_computation.4 | loop fusion | flops 25141248 | bytes 37797888 | tf_op jit(solution)/shard_map/reduce_sum | solution.py:12
  13.5 32.8 %all-gather = bf16[256,768]{1,0:T(8,128)(2,1)S(1)} all-gather(bf16[32,768]{1,0:T(8,128)(2,1)S(1)} %multiply_reduce_fusion.1), channel_id=2, replica_groups=mesh['bank'=4,'zero'=8] {'zero'}, dimensions={0}, use_global_device_ids=true | all-gather | bytes 442368 | tf_op jit(solution)/shard_map/all_gather | solution.py:12
  46.3 0.1 reduce_sum.31
  46.4 17.2 %divide_convert_fusion.1 = bf16[32,256,768]{2,1,0:T(8,128)(2,1)} fusion(f32[32,256,768]{2,1,0:T(8,128)} %param.6, bf16[32,256,768]{2,1,0:T(8,128)(2,1)} %param.7, f32[32,768]{1,0:T(8,128)S(1)} %convert_sqrt_fusion.1), kind=kLoop, calls=%fused_computation.3 | loop fusion | flops 25165824 | bytes 50429952 | tf_op jit(solution)/shard_map/convert_element_type | solution.py:22
  63.6 5.6 all-to-all-start
  69.2 12.8 %multiply_reduce_fusion = bf16[32,768]{1,0:T(8,128)(2,1)S(1)} fusion(f32[32,256,768]{2,1,0:T(8,128)} %param.8, bf16[32,256,768]{2,1,0:T(8,128)(2,1)} %param.9), kind=kLoop, calls=%fused_computation.1 | loop fusion | flops 25141248 | bytes 37797888 | tf_op jit(solution)/shard_map/reduce_sum | solution.py:15
  82.0 277.7 %psum.7 = bf16[32,768]{1,0:T(8,128)(2,1)S(1)} all-reduce(bf16[32,768]{1,0:T(8,128)(2,1)S(1)} %multiply_reduce_fusion), channel_id=1, replica_groups=mesh['bank'=4,'zero'=8] {'zero'}, use_global_device_ids=true, to_apply=%region_3.0 | all-reduce | flops 24576 | bytes 98304 | tf_op jit(solution)/shard_map/psum | solution.py:15
  359.8 17.4 %divide_convert_fusion = bf16[32,256,768]{2,1,0:T(8,128)(2,1)} fusion(f32[32,256,768]{2,1,0:T(8,128)} %param.8, bf16[32,256,768]{2,1,0:T(8,128)(2,1)} %param.9, f32[32,768]{1,0:T(8,128)S(1)} %convert_sqrt_fusion), kind=kLoop, calls=%fused_computation | loop fusion | flops 25165824 | bytes 50429952 | tf_op jit(solution)/shard_map/convert_element_type | solution.py:23
  377.2 0.0 copy-start
  377.2 0.0 copy-start.1
  377.2 0.0 all-to-all-done
  377.2 5.5 all-to-all-start.1
  382.7 0.0 copy-done
  382.8 0.0 copy-done.1
  382.8 286.1 %all_gather.11 = bf16[2048,32]{0,1:T(8,128)(2,1)S(1)} all-gather(bf16[256,32]{0,1:T(8,128)(2,1)S(1)} %multiply_convert_fusion), channel_id=1, replica_groups=mesh['bank'=4,'zero'=8] {'zero'}, dimensions={0}, use_global_device_ids=true | all-gather | bytes 147456 | tf_op jit(solution)/shard_map/all_gather | solution.py:36
  668.9 7.2 %all_gather.12 = bf16[2048,128]{0,1:T(8,128)(2,1)S(1)} all-gather(bf16[2048,32]{0,1:T(8,128)(2,1)S(1)} %all_gather.11), channel_id=1, replica_groups=mesh['bank'=4,'zero'=8] {'bank'}, dimensions={1}, use_global_device_ids=true | all-gather | bytes 655360 | tf_op jit(solution)/shard_map/all_gather | solution.py:37
  676.0 1.0 copy.19
  677.0 0.6 constant_dynamic-slice_fusion.1
  677.7 0.6 constant_dynamic-slice_fusion
  678.3 10.7 %copy.17 = bf16[8,4,256,768]{3,2,0,1:T(8,128)(2,1)} copy(bf16[8,4,256,768]{3,2,1,0:T(8,128)(2,1)} %bitcast.1) | data formatting | bytes 25165824 | tf_op jit(solution)/shard_map/all_to_all | solution.py:26
  688.9 0.0 all-to-all-done.1
  688.9 10.7 %copy.18 = bf16[8,4,256,768]{3,2,0,1:T(8,128)(2,1)} copy(bf16[8,4,256,768]{3,2,1,0:T(8,128)(2,1)} %bitcast.4) | data formatting | bytes 25165824 | tf_op jit(solution)/shard_map/all_to_all | solution.py:27
  (3 shorter events, 0.1 us)
Async XLA Ops:
  63.6 313.6 %all-to-all-start = ((bf16[32,256,768]{2,1,0:T(8,128)(2,1)}), bf16[32,256,768]{2,1,0:T(8,128)(2,1)}, u32[]{:S(2)}, u32[]{:S(2)}) async-start(bf16[32,256,768]{2,1,0:T(8,128)(2,1)} %divide_convert_fusion.1), calls=%async_computation | async-start | bytes 25165824 | tf_op jit(solution)/shard_map/all_to_all | solution.py:26
  377.2 5.6 copy-start
  377.2 5.6 copy-start.1
  377.2 311.7 %all-to-all-start.1 = ((bf16[32,256,768]{2,1,0:T(8,128)(2,1)}), bf16[32,256,768]{2,1,0:T(8,128)(2,1)}, u32[]{:S(2)}, u32[]{:S(2)}) async-start(bf16[32,256,768]{2,1,0:T(8,128)(2,1)} %divide_convert_fusion), calls=%async_computation.1 | async-start | bytes 25165824 | tf_op jit(solution)/shard_map/all_to_all | solution.py:27
